TPU v7x, 32 devices: a whole 2x2x4 slice. The times are simulated.
32 devices in a mesh: section: 4 (over y, core), tensor: 8 (over z, x).
Axes of the slice: x: 2, y: 2, z: 4, core: 2. Of those that a mesh axis runs over, the one named last changes fastest.
Arguments:
- saved_inputs: bfloat16 [4, 4, 256, 1024], P('section', None, 'tensor'), may hold values from -6 to 6
- slot_index: int32 [4, 3], P('section'), may hold values from 0 to 3
- example_lengths: int32 [4, 3, 2], P('section'), may hold values from 1 to 192, 256 in all within a row
- first_grads: bfloat16 [4, 256, 1024], P('section', 'tensor'), may hold values from -6 to 6
- loss_grads: bfloat16 [2, 256, 1024], P(None, 'tensor'), may hold values from -6 to 6
- w_in: bfloat16 [4, 1024, 32768], P('section', None, 'tensor'), may hold values from -0.1875 to 0.1875
- w_out: bfloat16 [4, 32768, 1024], P('section', 'tensor'), may hold values from -0.03125 to 0.03125
Outputs:
- grad_in: bfloat16 [4, 1024, 32768], P('section', None, 'tensor')
- grad_out: bfloat16 [4, 32768, 1024], P('section', 'tensor')
- input_grads: bfloat16 [4, 3, 256, 1024], P('section', None, 'tensor')
Inputs may be any that keep to these rules, and one draw needn't show every extreme that they name: `example_lengths`: the 2 lengths of one microbatch sum to 256.
All inputs are finite; a program needn't handle non-finite values.
Results may differ from a plain program's by a relative error of at most 0.0095.
Values may be sent and summed in bfloat16 or wider, within the bound.
A program may use at most 128 MiB of HBM per device.

v0:
```python
import jax
import jax.numpy as jnp
from jax import lax
from jax.sharding import PartitionSpec as P

D = 1024
FF = 32768
GAMMA = 0.01


def shifted(value, axis, steps):
    count = lax.axis_size(axis)
    first, last = (max(0, -steps), min(count, count - steps))
    return lax.ppermute(value, axis, [(source, source + steps) for source in range(first, last)])


def membership(lengths, tokens):
    ends = jnp.cumsum(lengths)
    position = jnp.arange(tokens, dtype=jnp.int32)
    example_id = jnp.sum((position[:, None] >= ends[None, :-1]).astype(jnp.int32), axis=1)
    labels = jnp.arange(lengths.shape[0], dtype=jnp.int32)
    return (example_id[:, None] == labels[None, :]).astype(jnp.float32)


def per_device(saved_inputs, slot_index, example_lengths, first_grads, loss_grads, w_in, w_out):
    section_count = lax.axis_size("section")
    is_last = lax.axis_index("section") == section_count - 1
    first = w_in[0]
    second = w_out[0]
    slot_count = loss_grads.shape[0] + 1
    rows = first_grads.shape[1]
    picked = [
        lax.dynamic_index_in_dim(saved_inputs[0], slot_index[0, slot], 0, keepdims=False)
        for slot in range(slot_count)
    ]
    every_input = lax.all_gather(jnp.stack(picked), "tensor", axis=1, tiled=True)
    acc_first = jnp.zeros(first.shape, jnp.float32)
    acc_second = jnp.zeros(second.shape, jnp.float32)
    incoming = first_grads[0]
    results = []
    for slot in range(slot_count):
        inputs = every_input[slot]
        grads = lax.all_gather(incoming, "tensor", axis=0, tiled=True)
        z = jnp.dot(inputs, first, preferred_element_type=jnp.float32)
        relu = jnp.maximum(z, 0.0)
        hidden = (relu * relu).astype(jnp.bfloat16)
        back = jnp.einsum("td,fd->tf", grads, second, preferred_element_type=jnp.float32)
        dz = (2.0 * relu * back).astype(jnp.bfloat16)
        own_terms = jnp.einsum("tf,df->td", dz, first, preferred_element_type=jnp.float32)
        summed = lax.psum(own_terms, "tensor")
        shares = lax.dynamic_slice_in_dim(summed, lax.axis_index("tensor") * rows, rows, 0)
        member = membership(example_lengths[0, slot], inputs.shape[0])
        pieces = []
        for example in range(member.shape[1]):
            keep = member[:, example][:, None].astype(jnp.bfloat16)
            per_first = jnp.einsum(
                "td,tf->df", inputs * keep, dz, preferred_element_type=jnp.float32
            )
            per_second = jnp.einsum(
                "tf,td->fd", hidden, grads * keep, preferred_element_type=jnp.float32
            )
            pieces.append(jnp.sum(per_first * per_first) + jnp.sum(per_second * per_second))
        local_squares = jnp.stack(pieces)
        squares = lax.psum(local_squares, "tensor")
        factor = 1.0 / (jnp.sqrt(squares / (D * FF)) + GAMMA)
        token_factor = jnp.sum(member * factor[None, :], axis=1)
        dzc = (dz.astype(jnp.float32) * token_factor[:, None]).astype(jnp.bfloat16)
        dyc = (grads.astype(jnp.float32) * token_factor[:, None]).astype(jnp.bfloat16)
        acc_first = acc_first + jnp.einsum(
            "td,tf->df", inputs, dzc, preferred_element_type=jnp.float32
        )
        acc_second = acc_second + jnp.einsum(
            "tf,td->fd", hidden, dyc, preferred_element_type=jnp.float32
        )
        passing = (incoming.astype(jnp.float32) + shares).astype(jnp.bfloat16)
        results.append(passing)
        if slot + 1 < slot_count:
            arrived = shifted(passing, "section", -1)
            incoming = jnp.where(is_last, loss_grads[slot], arrived)
    grad_in = acc_first.astype(jnp.bfloat16)[None]
    grad_out = acc_second.astype(jnp.bfloat16)[None]
    input_grads = jnp.stack(results)[None]
    return (grad_in, grad_out, input_grads)


def solution(mesh):
    return jax.shard_map(
        per_device,
        mesh=mesh,
        in_specs=(
            P("section", None, "tensor", None),
            P("section", None),
            P("section", None, None),
            P("section", "tensor", None),
            P(None, "tensor", None),
            P("section", None, "tensor"),
            P("section", "tensor", None),
        ),
        out_specs=(
            P("section", None, "tensor"),
            P("section", "tensor", None),
            P("section", None, "tensor", None),
        ),
        check_vma=False,
    )
```

profile of v0, /device:TPU:0, one launch (start us, length us, event | category | flops | bytes accessed | tf_op | source)
XLA Modules:
  0.0 492.9 jit_solution(11279649531270042013)
XLA Ops:
  7.2 1.4 fusion.83
  14.4 0.9 dynamic-slice_bitcast_fusion.2
  15.3 0.7 pad_maximum_fusion
  16.1 1.0 slice_reduce_fusion.6
  17.9 34.0 %all-gather = bf16[1,256,1024]{2,1,0:T(8,128)(2,1)S(1)} all-gather(bf16[1,32,1024]{2,1,0:T(8,128)(2,1)} %param.10), channel_id=2, replica_groups=mesh['section'=4,'tensor'=8] {'tensor'}, dimensions={1}, use_global_device_ids=true | all-gather | bytes 589824 | tf_op jit(solution)/shard_map/all_gather | solution.py:43
  51.9 12.3 %all-gather.3.cloned.1.call-done = bf16[3,256,1024]{2,1,0:T(8,128)(2,1)} async-done(((bf16[3,32,1024]{2,1,0:T(8,128)(2,1)}), bf16[3,256,1024]{2,1,0:T(8,128)(2,1)}) %all-gather.3.cloned.1.call-update) | async-done | bytes 1572880 | tf_op jit(solution)/shard_map/all_gather | solution.py:36
  64.2 5.9 %fusion.20 = f32[256,4096]{1,0:T(8,128)S(1)} fusion(bf16[1,1024,4096]{2,1,0:T(8,128)(2,1)} %param.12, bf16[3,256,1024]{2,1,0:T(8,128)(2,1)} %all-gather.3.cloned.1.call-done), kind=kOutput, calls=%fused_computation.34 | convolution fusion | flops 2148532224 | bytes 13107200 | tf_op jit(solution)/shard_map/dot_general | solution.py:44
  70.2 5.2 %multiply_reduce_fusion.8 = f32[]{:T(128)} fusion(bf16[1,256,1024]{2,1,0:T(8,128)(2,1)S(1)} %all-gather, bf16[256]{0:T(256)(128)(2,1)S(1)} %get-tuple-element.11, f32[256,4096]{1,0:T(8,128)S(1)} %fusion.20), kind=kOutput, calls=%fused_computation.10 | convolution fusion | flops 2158231552 | bytes 4719108 | tf_op jit(solution)/shard_map/tf,td->fd/dot_general | solution.py:59
  75.4 5.2 %multiply_reduce_fusion.10 = f32[]{:T(128)} fusion(bf16[1,256,1024]{2,1,0:T(8,128)(2,1)S(1)} %all-gather, bf16[256]{0:T(256)(128)(2,1)S(1)} %get-tuple-element.10, f32[256,4096]{1,0:T(8,128)S(1)} %fusion.20), kind=kOutput, calls=%fused_computation.12 | convolution fusion | flops 2158231552 | bytes 4719108 | tf_op jit(solution)/shard_map/tf,td->fd/dot_general | solution.py:59
  80.6 13.6 %fusion.44 = bf16[256,4096]{1,0:T(8,128)(2,1)S(1)} fusion(bf16[1,4096,1024]{2,1,0:T(8,128)(2,1)S(1)} %bitcast.137, f32[256,4096]{1,0:T(8,128)S(1)} %fusion.20, bf16[1,256,1024]{2,1,0:T(8,128)(2,1)S(1)} %all-gather), kind=kOutput, calls=%fused_computation.42 | convolution fusion | flops 2150629376 | bytes 15204352 | tf_op jit(solution)/shard_map/td,fd->tf/dot_general | solution.py:47
  94.2 7.5 %fusion.12 = f32[256,1024]{1,0:T(8,128)} fusion(bf16[256,4096]{1,0:T(8,128)(2,1)S(1)} %fusion.44, bf16[1,1024,4096]{2,1,0:T(8,128)(2,1)} %param.12), kind=kOutput, calls=%fused_computation.26 | convolution fusion | flops 2147483648 | bytes 11534336 | tf_op jit(solution)/shard_map/tf,df->td/dot_general | solution.py:49
  101.8 6.3 %multiply_reduce_fusion.9 = f32[]{:T(128)} fusion(bf16[256,4096]{1,0:T(8,128)(2,1)S(1)} %fusion.44, bf16[3,256,1024]{2,1,0:T(8,128)(2,1)} %all-gather.3.cloned.1.call-done, bf16[256]{0:T(256)(128)(2,1)S(1)} %get-tuple-element.11), kind=kOutput, calls=%fused_computation.11 | convolution fusion | flops 2156134400 | bytes 2621956 | tf_op jit(solution)/shard_map/td,tf->df/dot_general | solution.py:56
  109.4 6.3 %multiply_reduce_fusion.11 = f32[]{:T(128)} fusion(bf16[256,4096]{1,0:T(8,128)(2,1)S(1)} %fusion.44, bf16[3,256,1024]{2,1,0:T(8,128)(2,1)} %all-gather.3.cloned.1.call-done, bf16[256]{0:T(256)(128)(2,1)S(1)} %get-tuple-element.10), kind=kOutput, calls=%fused_computation.13 | convolution fusion | flops 2156134400 | bytes 2621956 | tf_op jit(solution)/shard_map/td,tf->df/dot_general | solution.py:56
  117.0 8.0 %fusion.26 = f32[256,4096]{1,0:T(8,128)} fusion(bf16[1,1024,4096]{2,1,0:T(8,128)(2,1)} %param.12, bf16[3,256,1024]{2,1,0:T(8,128)(2,1)} %all-gather.3.cloned.1.call-done), kind=kOutput, calls=%fused_computation.36 | convolution fusion | flops 2148532224 | bytes 13107200 | tf_op jit(solution)/shard_map/dot_general | solution.py:44
  125.0 8.5 %fusion.23 = f32[256,4096]{1,0:T(8,128)} fusion(bf16[1,1024,4096]{2,1,0:T(8,128)(2,1)} %param.12, bf16[3,256,1024]{2,1,0:T(8,128)(2,1)} %all-gather.3.cloned.1.call-done), kind=kOutput, calls=%fused_computation.35 | convolution fusion | flops 2148532224 | bytes 13107200 | tf_op jit(solution)/shard_map/dot_general | solution.py:44
  133.5 45.7 %all-reduce.5.cloned.1.call-done = f32[256,1024]{1,0:T(8,128)} async-done(((f32[256,1024]{1,0:T(8,128)}), f32[256,1024]{1,0:T(8,128)}) %all-reduce.5.cloned.1.call-update) | async-done | bytes 1048592 | tf_op jit(solution)/shard_map/psum | solution.py:50
  179.2 0.9 fusion.81
  180.1 1.3 collective-permute-start
  181.5 1.8 collective-permute-done
  183.2 31.3 %all_gather.14 = bf16[256,1024]{1,0:T(8,128)(2,1)S(1)} all-gather(bf16[32,1024]{1,0:T(8,128)(2,1)S(1)} %bitcast_select_fusion.1), channel_id=1, replica_groups=mesh['section'=4,'tensor'=8] {'tensor'}, dimensions={0}, use_global_device_ids=true | all-gather | bytes 589824 | tf_op jit(solution)/shard_map/all_gather | solution.py:43
  214.5 7.2 %fusion.41 = bf16[256,4096]{1,0:T(8,128)(2,1)S(1)} fusion(bf16[256,1024]{1,0:T(8,128)(2,1)S(1)} %all_gather.14, bf16[1,4096,1024]{2,1,0:T(8,128)(2,1)} %param.13, f32[256,4096]{1,0:T(8,128)} %fusion.23), kind=kOutput, calls=%fused_computation.41 | convolution fusion | flops 2150629376 | bytes 15204352 | tf_op jit(solution)/shard_map/td,fd->tf/dot_general | solution.py:47
  221.8 5.2 %multiply_reduce_fusion.4 = f32[]{:T(128)} fusion(bf16[256,1024]{1,0:T(8,128)(2,1)S(1)} %all_gather.14, bf16[256]{0:T(256)(128)(2,1)S(1)} %get-tuple-element.9, f32[256,4096]{1,0:T(8,128)S(1)} %copy-done.2), kind=kOutput, calls=%fused_computation.6 | convolution fusion | flops 2158231552 | bytes 4719108 | tf_op jit(solution)/shard_map/tf,td->fd/dot_general | solution.py:59
  226.9 6.8 %fusion.8 = f32[256,1024]{1,0:T(8,128)} fusion(bf16[256,4096]{1,0:T(8,128)(2,1)S(1)} %fusion.41, bf16[1,1024,4096]{2,1,0:T(8,128)(2,1)} %param.12), kind=kOutput, calls=%fused_computation.22 | convolution fusion | flops 2147483648 | bytes 11534336 | tf_op jit(solution)/shard_map/tf,df->td/dot_general | solution.py:49
  233.7 0.2 all-reduce.9.cloned.1.call-start
  234.0 6.3 %multiply_reduce_fusion.5 = f32[]{:T(128)} fusion(bf16[256,4096]{1,0:T(8,128)(2,1)S(1)} %fusion.41, bf16[3,256,1024]{2,1,0:T(8,128)(2,1)} %all-gather.3.cloned.1.call-done, bf16[256]{0:T(256)(128)(2,1)S(1)} %get-tuple-element.9), kind=kOutput, calls=%fused_computation.7 | convolution fusion | flops 2156134400 | bytes 2621956 | tf_op jit(solution)/shard_map/td,tf->df/dot_general | solution.py:56
  241.5 6.5 %multiply_reduce_fusion.7 = f32[]{:T(128)} fusion(bf16[256,4096]{1,0:T(8,128)(2,1)S(1)} %fusion.41, bf16[3,256,1024]{2,1,0:T(8,128)(2,1)} %all-gather.3.cloned.1.call-done, bf16[256]{0:T(256)(128)(2,1)S(1)} %get-tuple-element.8), kind=kOutput, calls=%fused_computation.9 | convolution fusion | flops 2156134400 | bytes 2621956 | tf_op jit(solution)/shard_map/td,tf->df/dot_general | solution.py:56
  248.0 5.6 %multiply_reduce_fusion.6 = f32[]{:T(128)} fusion(bf16[256,1024]{1,0:T(8,128)(2,1)S(1)} %all_gather.14, bf16[256]{0:T(256)(128)(2,1)S(1)} %get-tuple-element.8, f32[256,4096]{1,0:T(8,128)S(1)} %copy-done.3), kind=kOutput, calls=%fused_computation.8 | convolution fusion | flops 2158231552 | bytes 4719108 | tf_op jit(solution)/shard_map/tf,td->fd/dot_general | solution.py:59
  254.9 57.6 %all-reduce.7.cloned.1.call-done = f32[256,1024]{1,0:T(8,128)} async-done(((f32[256,1024]{1,0:T(8,128)}), f32[256,1024]{1,0:T(8,128)}) %all-reduce.7.cloned.1.call-update) | async-done | bytes 1048592 | tf_op jit(solution)/shard_map/psum | solution.py:50
  312.5 0.9 add_convert_fusion.3
  313.4 1.3 collective-permute-start.1
  314.8 1.8 collective-permute-done.1
  316.6 31.3 %all_gather.15 = bf16[256,1024]{1,0:T(8,128)(2,1)S(1)} all-gather(bf16[32,1024]{1,0:T(8,128)(2,1)S(1)} %bitcast_select_fusion), channel_id=1, replica_groups=mesh['section'=4,'tensor'=8] {'tensor'}, dimensions={0}, use_global_device_ids=true | all-gather | bytes 589824 | tf_op jit(solution)/shard_map/all_gather | solution.py:43
  347.9 7.1 %fusion.38 = bf16[256,4096]{1,0:T(8,128)(2,1)S(1)} fusion(bf16[256,1024]{1,0:T(8,128)(2,1)S(1)} %all_gather.15, bf16[1,4096,1024]{2,1,0:T(8,128)(2,1)} %param.13, f32[256,4096]{1,0:T(8,128)} %fusion.26), kind=kOutput, calls=%fused_computation.40 | convolution fusion | flops 2150629376 | bytes 15204352 | tf_op jit(solution)/shard_map/td,fd->tf/dot_general | solution.py:47
  355.0 5.2 %multiply_reduce_fusion = f32[]{:T(128)} fusion(bf16[256,1024]{1,0:T(8,128)(2,1)S(1)} %all_gather.15, bf16[256]{0:T(256)(128)(2,1)S(1)} %get-tuple-element.4, f32[256,4096]{1,0:T(8,128)S(1)} %copy-done.4), kind=kOutput, calls=%fused_computation.2 | convolution fusion | flops 2158231552 | bytes 4719108 | tf_op jit(solution)/shard_map/tf,td->fd/dot_general | solution.py:59
  360.2 5.2 %multiply_reduce_fusion.2 = f32[]{:T(128)} fusion(bf16[256,1024]{1,0:T(8,128)(2,1)S(1)} %all_gather.15, bf16[256]{0:T(256)(128)(2,1)S(1)} %get-tuple-element.3, f32[256,4096]{1,0:T(8,128)S(1)} %copy-done.4), kind=kOutput, calls=%fused_computation.4 | convolution fusion | flops 2158231552 | bytes 4719108 | tf_op jit(solution)/shard_map/tf,td->fd/dot_general | solution.py:59
  365.4 6.5 %multiply_reduce_fusion.1 = f32[]{:T(128)} fusion(bf16[256,4096]{1,0:T(8,128)(2,1)S(1)} %fusion.38, bf16[3,256,1024]{2,1,0:T(8,128)(2,1)} %all-gather.3.cloned.1.call-done, bf16[256]{0:T(256)(128)(2,1)S(1)} %get-tuple-element.4), kind=kOutput, calls=%fused_computation.3 | convolution fusion | flops 2156134400 | bytes 2621956 | tf_op jit(solution)/shard_map/td,tf->df/dot_general | solution.py:56
  373.1 6.3 %multiply_reduce_fusion.3 = f32[]{:T(128)} fusion(bf16[256,4096]{1,0:T(8,128)(2,1)S(1)} %fusion.38, bf16[3,256,1024]{2,1,0:T(8,128)(2,1)} %all-gather.3.cloned.1.call-done, bf16[256]{0:T(256)(128)(2,1)S(1)} %get-tuple-element.3), kind=kOutput, calls=%fused_computation.5 | convolution fusion | flops 2156134400 | bytes 2621956 | tf_op jit(solution)/shard_map/td,tf->df/dot_general | solution.py:56
  380.7 6.7 %fusion.6 = f32[256,1024]{1,0:T(8,128)} fusion(bf16[256,4096]{1,0:T(8,128)(2,1)S(1)} %fusion.38, bf16[1,1024,4096]{2,1,0:T(8,128)(2,1)} %param.12), kind=kOutput, calls=%fused_computation.20 | convolution fusion | flops 2147483648 | bytes 11534336 | tf_op jit(solution)/shard_map/tf,df->td/dot_general | solution.py:49
  387.5 20.4 %all-reduce = (f32[2]{0:T(128)S(1)}, f32[2]{0:T(128)S(1)}, f32[2]{0:T(128)S(1)}) all-reduce(f32[2]{0:T(128)S(1)} %pad_maximum_fusion.1, f32[2]{0:T(128)S(1)} %pad_maximum_fusion.2, f32[2]{0:T(128)S(1)} %pad_maximum_fusion.3), channel_id=1, replica_groups=mesh['section'=4,'tensor'=8] {'tensor'}, use_global_device_ids=true, to_apply=%region_5.6 | all-reduce | flops 6 | bytes 48 | tf_op jit(solution)/shard_map/psum | solution.py:64
  408.2 10.6 %fusion.53 = f32[4096,1024]{1,0:T(8,128)} fusion(bf16[256,1024]{1,0:T(8,128)(2,1)} %copy-done.5, f32[256]{0:T(256)S(1)} %select_reduce_fusion.1, f32[256,4096]{1,0:T(8,128)} %fusion.23), kind=kOutput, calls=%fused_computation.58 | convolution fusion | flops 2150367232 | bytes 21496832 | tf_op jit(solution)/shard_map/tf,td->fd/dot_general | solution.py:72
  418.8 8.2 %fusion.52 = f32[4096,1024]{1,0:T(8,128)} fusion(bf16[1,256,1024]{2,1,0:T(8,128)(2,1)S(1)} %all-gather, f32[256]{0:T(256)S(1)} %select_reduce_fusion.2, f32[256,4096]{1,0:T(8,128)S(1)} %copy-done.1), kind=kOutput, calls=%fused_computation.57 | convolution fusion | flops 2150367232 | bytes 21496832 | tf_op jit(solution)/shard_map/tf,td->fd/dot_general | solution.py:72
  427.0 16.7 %fusion.19 = bf16[1,4096,1024]{2,1,0:T(8,128)(2,1)} fusion(f32[4096,1024]{1,0:T(8,128)} %fusion.52, f32[4096,1024]{1,0:T(8,128)} %fusion.53, bf16[256,1024]{1,0:T(8,128)(2,1)S(1)} %all_gather.15, f32[256]{0:T(256)S(1)} %select_reduce_fusion, f32[256,4096]{1,0:T(8,128)} %fusion.26), kind=kOutput, calls=%fused_computation.33 | convolution fusion | flops 2162950144 | bytes 46662656 | tf_op jit(solution)/shard_map/tf,td->fd/dot_general | solution.py:72
  443.8 10.1 %fusion.47 = f32[1024,4096]{1,0:T(8,128)} fusion(bf16[256,4096]{1,0:T(8,128)(2,1)} %copy-done.6, f32[256]{0:T(256)S(1)} %select_reduce_fusion.2, bf16[3,256,1024]{2,1,0:T(8,128)(2,1)} %all-gather.3.cloned.1.call-done), kind=kOutput, calls=%fused_computation.49 | convolution fusion | flops 2150629376 | bytes 19399680 | tf_op jit(solution)/shard_map/td,tf->df/dot_general | solution.py:69
  453.9 9.3 %fusion.48 = f32[1024,4096]{1,0:T(8,128)} fusion(bf16[256,4096]{1,0:T(8,128)(2,1)S(1)} %copy-done.8, f32[256]{0:T(256)S(1)} %select_reduce_fusion.1, bf16[3,256,1024]{2,1,0:T(8,128)(2,1)} %all-gather.3.cloned.1.call-done), kind=kOutput, calls=%fused_computation.50 | convolution fusion | flops 2150629376 | bytes 19399680 | tf_op jit(solution)/shard_map/td,tf->df/dot_general | solution.py:69
  463.1 16.0 %fusion.18 = bf16[1,1024,4096]{2,1,0:T(8,128)(2,1)} fusion(f32[1024,4096]{1,0:T(8,128)} %fusion.47, f32[1024,4096]{1,0:T(8,128)} %fusion.48, bf16[256,4096]{1,0:T(8,128)(2,1)S(1)} %fusion.38, f32[256]{0:T(256)S(1)} %select_reduce_fusion, bf16[3,256,1024]{2,1,0:T(8,128)(2,1)} %all-gather.3.cloned.1.call-done), kind=kOutput, calls=%fused_computation.32 | convolution fusion | flops 2163212288 | bytes 44565504 | tf_op jit(solution)/shard_map/td,tf->df/dot_general | solution.py:69
  479.2 5.2 %all-reduce.9.cloned.1.call-done = f32[256,1024]{1,0:T(8,128)} async-done(((f32[256,1024]{1,0:T(8,128)}), f32[256,1024]{1,0:T(8,128)}) %all-reduce.9.cloned.1.call-update) | async-done | bytes 1048592 | tf_op jit(solution)/shard_map/psum | solution.py:50
  484.3 0.9 fusion.82
  485.2 0.7 maximum_bitcast_fusion
  (56 shorter events, 1.5 us)
Async XLA Ops:
  7.2 57.0 %all-gather.3.cloned.1.call-start = ((), (), s32[]{:S(2)}) async-start(), calls=%async_computation | async-start | bytes 1769472 | tf_op jit(solution)/shard_map/all_gather | solution.py:36
  16.0 163.1 %all-reduce.5.cloned.1.call-start = ((), (), s32[]{:S(2)}) async-start(), calls=%async_computation.1 | async-start | bytes 2097152 | tf_op jit(solution)/shard_map/psum | solution.py:50
  70.1 10.4 %copy-start = (f32[256,4096]{1,0:T(8,128)}, f32[256,4096]{1,0:T(8,128)S(1)}, u32[]{:S(2)}) copy-start(f32[256,4096]{1,0:T(8,128)S(1)} %fusion.20) | copy-start | bytes 12582916
  70.2 10.4 %slice-start = ((s8[8388608]{0:T(1024)(128)(4,1)}), s8[4194304]{0:T(1024)(128)(4,1)S(1)}, s32[]{:S(2)}) async-start(s8[8388608]{0:T(1024)(128)(4,1)} %bitcast.136), calls=%async_computation.4 | async-start | bytes 8388608
  75.4 5.2 %slice-start.1 = ((s8[8388608]{0:T(1024)(128)(4,1)}), s8[4194304]{0:T(1024)(128)(4,1)S(1)}, s32[]{:S(2)}) async-start(s8[8388608]{0:T(1024)(128)(4,1)} %bitcast.136), calls=%async_computation.5 | async-start | bytes 8388608
  94.2 15.2 %copy-start.6 = (bf16[256,4096]{1,0:T(8,128)(2,1)}, bf16[256,4096]{1,0:T(8,128)(2,1)S(1)}, u32[]{:S(2)}) copy-start(bf16[256,4096]{1,0:T(8,128)(2,1)S(1)} %fusion.44) | copy-start | bytes 6291460
  101.7 210.8 %all-reduce.7.cloned.1.call-start = ((), (), s32[]{:S(2)}) async-start(), calls=%async_computation.2 | async-start | bytes 2097152 | tf_op jit(solution)/shard_map/psum | solution.py:50
  125.0 54.2 %copy-start.9 = (bf16[1,32,1024]{2,1,0:T(8,128)(2,1)S(1)}, bf16[1,32,1024]{2,1,0:T(8,128)(2,1)}, u32[]{:S(2)}) copy-start(bf16[1,32,1024]{2,1,0:T(8,128)(2,1)} %param.10) | copy-start | bytes 196612
  125.0 58.3 %copy-start.10 = (bf16[2,32,1024]{2,1,0:T(8,128)(2,1)S(1)}, bf16[2,32,1024]{2,1,0:T(8,128)(2,1)}, u32[]{:S(2)}) copy-start(bf16[2,32,1024]{2,1,0:T(8,128)(2,1)} %param.11) | copy-start | bytes 393220
  180.1 3.1 collective-permute-start
  214.5 33.5 %copy-start.5 = (bf16[256,1024]{1,0:T(8,128)(2,1)}, bf16[256,1024]{1,0:T(8,128)(2,1)S(1)}, u32[]{:S(2)}) copy-start(bf16[256,1024]{1,0:T(8,128)(2,1)S(1)} %all_gather.14) | copy-start | bytes 1572868
  214.5 7.2 %copy-start.2 = (f32[256,4096]{1,0:T(8,128)S(1)}, f32[256,4096]{1,0:T(8,128)}, u32[]{:S(2)}) copy-start(f32[256,4096]{1,0:T(8,128)} %fusion.23) | copy-start | bytes 12582916
  221.7 19.7 %copy-start.7 = (bf16[256,4096]{1,0:T(8,128)(2,1)}, bf16[256,4096]{1,0:T(8,128)(2,1)S(1)}, u32[]{:S(2)}) copy-start(bf16[256,4096]{1,0:T(8,128)(2,1)S(1)} %fusion.41) | copy-start | bytes 6291460
  233.7 250.6 %all-reduce.9.cloned.1.call-start = ((), (), s32[]{:S(2)}) async-start(), calls=%async_computation.3 | async-start | bytes 2097152 | tf_op jit(solution)/shard_map/psum | solution.py:50
  241.5 6.5 %copy-start.3 = (f32[256,4096]{1,0:T(8,128)S(1)}, f32[256,4096]{1,0:T(8,128)}, u32[]{:S(2)}) copy-start(f32[256,4096]{1,0:T(8,128)} %fusion.23) | copy-start | bytes 12582916
  313.4 3.1 collective-permute-start.1
  347.9 7.1 %copy-start.4 = (f32[256,4096]{1,0:T(8,128)S(1)}, f32[256,4096]{1,0:T(8,128)}, u32[]{:S(2)}) copy-start(f32[256,4096]{1,0:T(8,128)} %fusion.26) | copy-start | bytes 12582916
  408.2 10.6 %copy-start.1 = (f32[256,4096]{1,0:T(8,128)S(1)}, f32[256,4096]{1,0:T(8,128)}, u32[]{:S(2)}) copy-start(f32[256,4096]{1,0:T(8,128)} %copy-done) | copy-start | bytes 12582916
  443.8 10.1 %copy-start.8 = (bf16[256,4096]{1,0:T(8,128)(2,1)S(1)}, bf16[256,4096]{1,0:T(8,128)(2,1)}, u32[]{:S(2)}) copy-start(bf16[256,4096]{1,0:T(8,128)(2,1)} %copy-done.7) | copy-start | bytes 6291460
Sparse Core Ops, SparseCore 0:
  16.2 48.0 all-gather.2
  101.8 77.2 all-reduce.4
  233.8 78.5 all-reduce.6
  408.3 75.9 all-reduce.8
where the time goes:
time: 503 us; the launch traced here: 493 us
  matrix products  212 us (42%)
  waiting for transfers between devices  124 us (25%)
  blocking collectives  117 us (23%)
  between operations  27.8 us (6%)
  other arithmetic  5.36 us (1%)
    psum x3, waiting for transfers between devices, per_device(): summed = lax.psum(own_terms, 'tensor')  108 us
    all_gather x3, blocking collectives, per_device(): grads = lax.all_gather(incoming, 'tensor', axis=0, tiled=True)  96.6 us
    dot_general x6, matrix products, per_device(): jnp.einsum('td,tf->df', inputs * keep, dz, preferred_element_type=jnp.flo...  38.2 us
    dot_general x3, matrix products, per_device(): jnp.einsum('tf,td->fd', hidden, dyc, preferred_element_type=jnp.float32)  35.6 us
    dot_general x3, matrix products, per_device(): jnp.einsum('td,tf->df', inputs, dzc, preferred_element_type=jnp.float32)  35.4 us
    dot_general x6, matrix products, per_device(): jnp.einsum('tf,td->fd', hidden, grads * keep, preferred_element_type=jnp....  31.6 us
    dot_general x3, matrix products, per_device(): jnp.einsum('td,fd->tf', grads, second, preferred_element_type=jnp.float32)  27.9 us
    dot_general x3, matrix products, per_device(): z = jnp.dot(inputs, first, preferred_element_type=jnp.float32)  22.4 us
  transfers between devices with their start and end apart: 6, of which 6 were waited for; matrix products, arithmetic and copies ran while one was open for 24% of the time, Pallas kernels for 0%

commit v1 on v0

--- a/solution.py
+++ b/solution.py
@@ -47,7 +47,8 @@
         back = jnp.einsum("td,fd->tf", grads, second, preferred_element_type=jnp.float32)
         dz = (2.0 * relu * back).astype(jnp.bfloat16)
         own_terms = jnp.einsum("tf,df->td", dz, first, preferred_element_type=jnp.float32)
-        summed = lax.psum(own_terms, "tensor")
+        blocks = lax.all_gather(own_terms, "tensor", axis=0, tiled=False)
+        summed = blocks.sum(axis=0)
         shares = lax.dynamic_slice_in_dim(summed, lax.axis_index("tensor") * rows, rows, 0)
         member = membership(example_lengths[0, slot], inputs.shape[0])
         pieces = []

time: 503 us -> 626 us (1.24)
  waiting for transfers between devices: 124 us -> 259 us
  matrix products: 212 us -> 191 us
  other arithmetic: 5.36 us -> 15.9 us
    all_gather x0 -> x3, waiting for transfers between devices: none -> 246 us  [per_device(): blocks = lax.all_gather(own_terms, 'tensor', axis=0, tiled=False)]
    psum x3 -> x0, waiting for transfers between devices: 108 us -> none  [per_device(): summed = lax.psum(own_terms, 'tensor')]
    dot_general x3, matrix products: 27.9 us -> 12.2 us  [per_device(): jnp.einsum('td,fd->tf', grads, second, preferred_element_type=jnp.float32)]
    reduce_sum x0 -> x3, other arithmetic: none -> 13.2 us  [per_device(): summed = blocks.sum(axis=0)]
  transfers between devices with their start and end apart: 6 -> 6, of which waited for: 6 -> 3; matrix products, arithmetic and copies ran while one was open for 24% -> 25% of each run, Pallas kernels for 0% -> 0%
where the time goes in v1:
time: 626 us; the launch traced here: 619 us
  waiting for transfers between devices  259 us (41%)
  matrix products  191 us (31%)
  blocking collectives  117 us (19%)
  between operations  27.7 us (4%)
  other arithmetic  15.9 us (3%)
    all_gather x3, waiting for transfers between devices, per_device(): blocks = lax.all_gather(own_terms, 'tensor', axis=0, tiled=False)  246 us
    all_gather x3, blocking collectives, per_device(): grads = lax.all_gather(incoming, 'tensor', axis=0, tiled=True)  97.4 us
    dot_general x6, matrix products, per_device(): jnp.einsum('td,tf->df', inputs * keep, dz, preferred_element_type=jnp.flo...  41.9 us
    dot_general x3, matrix products, per_device(): jnp.einsum('td,tf->df', inputs, dzc, preferred_element_type=jnp.float32)  35.1 us
    dot_general x3, matrix products, per_device(): jnp.einsum('tf,td->fd', hidden, dyc, preferred_element_type=jnp.float32)  33.2 us
    dot_general x6, matrix products, per_device(): jnp.einsum('tf,td->fd', hidden, grads * keep, preferred_element_type=jnp....  32.3 us
    psum x1, blocking collectives, per_device(): squares = lax.psum(local_squares, 'tensor')  19.2 us
    dot_general x3, matrix products, per_device(): z = jnp.dot(inputs, first, preferred_element_type=jnp.float32)  19 us
  transfers between devices with their start and end apart: 6, of which 3 were waited for; matrix products, arithmetic and copies ran while one was open for 25% of the time, Pallas kernels for 0%

profile of v1, /device:TPU:0, one launch (start us, length us, event | category | flops | bytes accessed | tf_op | source)
XLA Modules:
  0.0 618.8 jit_solution(7736907273237496806)
XLA Ops:
  7.2 1.4 fusion.83
  14.4 0.9 dynamic-slice_bitcast_fusion.2
  15.3 0.7 pad_maximum_fusion
  16.1 34.0 %all-gather = bf16[1,256,1024]{2,1,0:T(8,128)(2,1)S(1)} all-gather(bf16[1,32,1024]{2,1,0:T(8,128)(2,1)} %param.10), channel_id=2, replica_groups=mesh['section'=4,'tensor'=8] {'tensor'}, dimensions={1}, use_global_device_ids=true | all-gather | bytes 589824 | tf_op jit(solution)/shard_map/all_gather | solution.py:43
  50.0 13.8 %all-gather.9.cloned.1.call-done = bf16[3,256,1024]{2,1,0:T(8,128)(2,1)} async-done(((bf16[3,32,1024]{2,1,0:T(8,128)(2,1)}), bf16[3,256,1024]{2,1,0:T(8,128)(2,1)}) %all-gather.9.cloned.1.call-update) | async-done | bytes 1572880 | tf_op jit(solution)/shard_map/all_gather | solution.py:36
  63.9 6.0 fusion.20
  70.0 7.4 %fusion.44 = bf16[256,4096]{1,0:T(8,128)(2,1)S(1)} fusion(bf16[1,4096,1024]{2,1,0:T(8,128)(2,1)} %param.13, f32[256,4096]{1,0:T(8,128)S(1)} %fusion.20, bf16[1,256,1024]{2,1,0:T(8,128)(2,1)S(1)} %all-gather), kind=kOutput, calls=%fused_computation.42 | convolution fusion | flops 2150629376 | bytes 15204352 | tf_op jit(solution)/shard_map/td,fd->tf/dot_general | solution.py:47
  77.4 1.3 copy-done.15
  78.7 3.3 fusion.12
  82.1 123.6 %all-gather.11.cloned.1.call-done = f32[2048,1024]{1,0:T(8,128)} async-done(((f32[256,1024]{1,0:T(8,128)}), f32[2048,1024]{1,0:T(8,128)}) %all-gather.11.cloned.1.call-update) | async-done | bytes 8388624 | tf_op jit(solution)/shard_map/all_gather | solution.py:50
  205.8 4.5 reduce_sum.179
  210.4 1.6 collective-permute-start
  211.9 6.5 %fusion.23 = f32[256,4096]{1,0:T(8,128)S(1)} fusion(bf16[1,1024,4096]{2,1,0:T(8,128)(2,1)} %param.12, bf16[3,256,1024]{2,1,0:T(8,128)(2,1)S(1)} %copy-done.18), kind=kOutput, calls=%fused_computation.35 | convolution fusion | flops 2148532224 | bytes 13107200 | tf_op jit(solution)/shard_map/dot_general | solution.py:44
  218.5 31.7 %all_gather.34 = bf16[256,1024]{1,0:T(8,128)(2,1)S(1)} all-gather(bf16[32,1024]{1,0:T(8,128)(2,1)S(1)} %bitcast_select_fusion.1), channel_id=1, replica_groups=mesh['section'=4,'tensor'=8] {'tensor'}, dimensions={0}, use_global_device_ids=true | all-gather | bytes 589824 | tf_op jit(solution)/shard_map/all_gather | solution.py:43
  250.2 2.4 fusion.41
  252.6 1.3 copy-done.16
  253.9 6.8 %fusion.8 = f32[256,1024]{1,0:T(8,128)} fusion(bf16[256,4096]{1,0:T(8,128)(2,1)S(1)} %fusion.41, bf16[1,1024,4096]{2,1,0:T(8,128)(2,1)} %param.12), kind=kOutput, calls=%fused_computation.22 | convolution fusion | flops 2147483648 | bytes 11534336 | tf_op jit(solution)/shard_map/tf,df->td/dot_general | solution.py:49
  260.8 0.2 slice_reduce_fusion.6
  261.0 0.2 reduce-window.14
  261.2 0.2 reduce-window.10
  261.7 121.9 %all-gather.13.cloned.1.call-done = f32[2048,1024]{1,0:T(8,128)} async-done(((f32[256,1024]{1,0:T(8,128)}), f32[2048,1024]{1,0:T(8,128)}) %all-gather.13.cloned.1.call-update) | async-done | bytes 8388624 | tf_op jit(solution)/shard_map/all_gather | solution.py:50
  383.6 4.4 reduce_sum.185
  388.0 1.6 collective-permute-start.1
  389.6 6.5 %fusion.26 = f32[256,4096]{1,0:T(8,128)S(1)} fusion(bf16[1,1024,4096]{2,1,0:T(8,128)(2,1)} %param.12, bf16[3,256,1024]{2,1,0:T(8,128)(2,1)S(1)} %copy-done.18), kind=kOutput, calls=%fused_computation.36 | convolution fusion | flops 2148532224 | bytes 13107200 | tf_op jit(solution)/shard_map/dot_general | solution.py:44
  396.1 31.7 %all_gather.37 = bf16[256,1024]{1,0:T(8,128)(2,1)S(1)} all-gather(bf16[32,1024]{1,0:T(8,128)(2,1)S(1)} %bitcast_select_fusion), channel_id=1, replica_groups=mesh['section'=4,'tensor'=8] {'tensor'}, dimensions={0}, use_global_device_ids=true | all-gather | bytes 589824 | tf_op jit(solution)/shard_map/all_gather | solution.py:43
  427.9 2.4 fusion.38
  430.3 6.8 %fusion.6 = f32[256,1024]{1,0:T(8,128)} fusion(bf16[256,4096]{1,0:T(8,128)(2,1)S(1)} %fusion.38, bf16[1,1024,4096]{2,1,0:T(8,128)(2,1)} %param.12), kind=kOutput, calls=%fused_computation.20 | convolution fusion | flops 2147483648 | bytes 11534336 | tf_op jit(solution)/shard_map/tf,df->td/dot_general | solution.py:49
  437.1 7.1 %multiply_reduce_fusion.9 = f32[]{:T(128)} fusion(bf16[256,4096]{1,0:T(8,128)(2,1)} %copy-done.15, bf16[3,256,1024]{2,1,0:T(8,128)(2,1)} %all-gather.9.cloned.1.call-done, bf16[256]{0:T(256)(128)(2,1)S(1)} %get-tuple-element.11), kind=kOutput, calls=%fused_computation.11 | convolution fusion | flops 2156134400 | bytes 2621956 | tf_op jit(solution)/shard_map/td,tf->df/dot_general | solution.py:57
  444.3 5.6 multiply_reduce_fusion.8
  451.2 7.2 %multiply_reduce_fusion.11 = f32[]{:T(128)} fusion(bf16[256,4096]{1,0:T(8,128)(2,1)} %copy-done.15, bf16[3,256,1024]{2,1,0:T(8,128)(2,1)} %all-gather.9.cloned.1.call-done, bf16[256]{0:T(256)(128)(2,1)S(1)} %get-tuple-element.10), kind=kOutput, calls=%fused_computation.13 | convolution fusion | flops 2156134400 | bytes 2621956 | tf_op jit(solution)/shard_map/td,tf->df/dot_general | solution.py:57
  458.3 5.2 multiply_reduce_fusion.10
  464.9 7.3 %multiply_reduce_fusion.5 = f32[]{:T(128)} fusion(bf16[256,4096]{1,0:T(8,128)(2,1)} %copy-done.16, bf16[3,256,1024]{2,1,0:T(8,128)(2,1)} %all-gather.9.cloned.1.call-done, bf16[256]{0:T(256)(128)(2,1)S(1)} %get-tuple-element.9), kind=kOutput, calls=%fused_computation.7 | convolution fusion | flops 2156134400 | bytes 2621956 | tf_op jit(solution)/shard_map/td,tf->df/dot_general | solution.py:57
  472.2 5.2 multiply_reduce_fusion.4
  478.7 7.4 %multiply_reduce_fusion.7 = f32[]{:T(128)} fusion(bf16[256,4096]{1,0:T(8,128)(2,1)} %copy-done.16, bf16[3,256,1024]{2,1,0:T(8,128)(2,1)} %all-gather.9.cloned.1.call-done, bf16[256]{0:T(256)(128)(2,1)S(1)} %get-tuple-element.8), kind=kOutput, calls=%fused_computation.9 | convolution fusion | flops 2156134400 | bytes 2621956 | tf_op jit(solution)/shard_map/td,tf->df/dot_general | solution.py:57
  486.1 5.2 multiply_reduce_fusion.6
  492.6 6.4 %multiply_reduce_fusion.1 = f32[]{:T(128)} fusion(bf16[256,4096]{1,0:T(8,128)(2,1)S(1)} %fusion.38, bf16[3,256,1024]{2,1,0:T(8,128)(2,1)} %all-gather.9.cloned.1.call-done, bf16[256]{0:T(256)(128)(2,1)S(1)} %get-tuple-element.4), kind=kOutput, calls=%fused_computation.3 | convolution fusion | flops 2156134400 | bytes 2621956 | tf_op jit(solution)/shard_map/td,tf->df/dot_general | solution.py:57
  499.1 5.7 multiply_reduce_fusion
  506.0 6.4 %multiply_reduce_fusion.3 = f32[]{:T(128)} fusion(bf16[256,4096]{1,0:T(8,128)(2,1)S(1)} %fusion.38, bf16[3,256,1024]{2,1,0:T(8,128)(2,1)} %all-gather.9.cloned.1.call-done, bf16[256]{0:T(256)(128)(2,1)S(1)} %get-tuple-element.3), kind=kOutput, calls=%fused_computation.5 | convolution fusion | flops 2156134400 | bytes 2621956 | tf_op jit(solution)/shard_map/td,tf->df/dot_general | solution.py:57
  512.5 5.4 multiply_reduce_fusion.2
  519.1 19.2 %all-reduce = (f32[2]{0:T(128)S(1)}, f32[2]{0:T(128)S(1)}, f32[2]{0:T(128)S(1)}) all-reduce(f32[2]{0:T(128)S(1)} %pad_maximum_fusion.1, f32[2]{0:T(128)S(1)} %pad_maximum_fusion.2, f32[2]{0:T(128)S(1)} %pad_maximum_fusion.3), channel_id=1, replica_groups=mesh['section'=4,'tensor'=8] {'tensor'}, use_global_device_ids=true, to_apply=%region_5.6 | all-reduce | flops 6 | bytes 48 | tf_op jit(solution)/shard_map/psum | solution.py:65
  538.6 10.1 %fusion.47 = f32[1024,4096]{1,0:T(8,128)} fusion(bf16[256,4096]{1,0:T(8,128)(2,1)} %copy-done.15, f32[256]{0:T(256)S(1)} %select_reduce_fusion.2, bf16[3,256,1024]{2,1,0:T(8,128)(2,1)} %all-gather.9.cloned.1.call-done), kind=kOutput, calls=%fused_computation.49 | convolution fusion | flops 2150629376 | bytes 19399680 | tf_op jit(solution)/shard_map/td,tf->df/dot_general | solution.py:70
  548.7 9.4 %fusion.48 = f32[1024,4096]{1,0:T(8,128)} fusion(bf16[256,4096]{1,0:T(8,128)(2,1)S(1)} %copy-done.17, f32[256]{0:T(256)S(1)} %select_reduce_fusion.1, bf16[3,256,1024]{2,1,0:T(8,128)(2,1)} %all-gather.9.cloned.1.call-done), kind=kOutput, calls=%fused_computation.50 | convolution fusion | flops 2150629376 | bytes 19399680 | tf_op jit(solution)/shard_map/td,tf->df/dot_general | solution.py:70
  558.1 8.2 %fusion.53 = f32[4096,1024]{1,0:T(8,128)} fusion(bf16[256,1024]{1,0:T(8,128)(2,1)S(1)} %copy-done.14, f32[256]{0:T(256)S(1)} %select_reduce_fusion.1, f32[256,4096]{1,0:T(8,128)S(1)} %copy-done.7), kind=kOutput, calls=%fused_computation.58 | convolution fusion | flops 2150367232 | bytes 21496832 | tf_op jit(solution)/shard_map/tf,td->fd/dot_general | solution.py:73
  566.3 8.2 %fusion.52 = f32[4096,1024]{1,0:T(8,128)} fusion(bf16[1,256,1024]{2,1,0:T(8,128)(2,1)S(1)} %all-gather, f32[256]{0:T(256)S(1)} %select_reduce_fusion.2, f32[256,4096]{1,0:T(8,128)S(1)} %copy-done.3), kind=kOutput, calls=%fused_computation.57 | convolution fusion | flops 2150367232 | bytes 21496832 | tf_op jit(solution)/shard_map/tf,td->fd/dot_general | solution.py:73
  574.5 15.6 %fusion.18 = bf16[1,1024,4096]{2,1,0:T(8,128)(2,1)} fusion(f32[1024,4096]{1,0:T(8,128)} %fusion.47, f32[1024,4096]{1,0:T(8,128)} %fusion.48, bf16[256,4096]{1,0:T(8,128)(2,1)S(1)} %fusion.38, f32[256]{0:T(256)S(1)} %select_reduce_fusion, bf16[3,256,1024]{2,1,0:T(8,128)(2,1)} %all-gather.9.cloned.1.call-done), kind=kOutput, calls=%fused_computation.32 | convolution fusion | flops 2163212288 | bytes 44565504 | tf_op jit(solution)/shard_map/td,tf->df/dot_general | solution.py:70
  590.1 16.8 %fusion.19 = bf16[1,4096,1024]{2,1,0:T(8,128)(2,1)} fusion(f32[4096,1024]{1,0:T(8,128)} %fusion.52, f32[4096,1024]{1,0:T(8,128)} %fusion.53, bf16[256,1024]{1,0:T(8,128)(2,1)S(1)} %all_gather.37, f32[256]{0:T(256)S(1)} %select_reduce_fusion, f32[256,4096]{1,0:T(8,128)} %copy-done.8), kind=kOutput, calls=%fused_computation.33 | convolution fusion | flops 2162950144 | bytes 46662656 | tf_op jit(solution)/shard_map/tf,td->fd/dot_general | solution.py:73
  606.9 4.4 reduce_sum.191
  611.4 0.7 maximum_bitcast_fusion
  (91 shorter events, 1.3 us)
Async XLA Ops:
  7.2 56.7 %all-gather.9.cloned.1.call-start = ((), (), s32[]{:S(2)}) async-start(), calls=%async_computation | async-start | bytes 1769472 | tf_op jit(solution)/shard_map/all_gather | solution.py:36
  16.0 189.7 %all-gather.11.cloned.1.call-start = ((), (), s32[]{:S(2)}) async-start(), calls=%async_computation.1 | async-start | bytes 9437184 | tf_op jit(solution)/shard_map/all_gather | solution.py:50
  63.9 14.8 %slice-start.4 = ((s8[8388608]{0:T(1024)(128)(4,1)}), s8[4194304]{0:T(1024)(128)(4,1)S(1)}, s32[]{:S(2)}) async-start(s8[8388608]{0:T(1024)(128)(4,1)} %bitcast.146), calls=%async_computation.8 | async-start | bytes 8388608
  69.9 7.4 %copy-start = (f32[256,4096]{1,0:T(8,128)}, f32[256,4096]{1,0:T(8,128)S(1)}, u32[]{:S(2)}) copy-start(f32[256,4096]{1,0:T(8,128)S(1)} %fusion.20) | copy-start | bytes 12582916
  70.0 8.8 %slice-start.5 = ((s8[8388608]{0:T(1024)(128)(4,1)}), s8[4194304]{0:T(1024)(128)(4,1)S(1)}, s32[]{:S(2)}) async-start(s8[8388608]{0:T(1024)(128)(4,1)} %bitcast.146), calls=%async_computation.9 | async-start | bytes 8388608
  77.4 1.4 copy-start.15
  82.1 301.5 %all-gather.13.cloned.1.call-start = ((), (), s32[]{:S(2)}) async-start(), calls=%async_computation.2 | async-start | bytes 9437184 | tf_op jit(solution)/shard_map/all_gather | solution.py:50
  205.8 4.5 copy-start.19
  205.8 6.1 copy-start.18
  210.3 39.9 %slice-start = ((s8[8388608]{0:T(1024)(128)(4,1)}), s8[4194304]{0:T(1024)(128)(4,1)S(1)}, s32[]{:S(2)}) async-start(s8[8388608]{0:T(1024)(128)(4,1)} %bitcast.142), calls=%async_computation.4 | async-start | bytes 8388608
  210.3 8.1 %copy-start.20 = (bf16[2,32,1024]{2,1,0:T(8,128)(2,1)S(1)}, bf16[2,32,1024]{2,1,0:T(8,128)(2,1)}, u32[]{:S(2)}) copy-start(bf16[2,32,1024]{2,1,0:T(8,128)(2,1)} %param.11) | copy-start | bytes 393220
  210.3 39.8 %slice-start.1 = ((s8[8388608]{0:T(1024)(128)(4,1)}), s8[4194304]{0:T(1024)(128)(4,1)S(1)}, s32[]{:S(2)}) async-start(s8[8388608]{0:T(1024)(128)(4,1)} %bitcast.142), calls=%async_computation.5 | async-start | bytes 8388608
  210.4 8.1 %collective-permute-start = (bf16[32,1024]{1,0:T(8,128)(2,1)S(1)}, bf16[32,1024]{1,0:T(8,128)(2,1)S(1)}, u32[]{:S(2)}, u32[]{:S(2)}) collective-permute-start(bf16[32,1024]{1,0:T(8,128)(2,1)S(1)} %fusion.81), channel_id=1, source_target_pairs={{8,0},{16,8},{24,16},{9,1},{17,9},{25,17},{10,2},{18,10},{26,18},{... | collective-permute-start | bytes 196616 | tf_op jit(solution)/shard_map/ppermute | solution.py:14
  218.4 34.1 %copy-start.4 = (f32[256,4096]{1,0:T(8,128)}, f32[256,4096]{1,0:T(8,128)S(1)}, u32[]{:S(2)}) copy-start(f32[256,4096]{1,0:T(8,128)S(1)} %fusion.23) | copy-start | bytes 12582916
  250.2 2.4 copy-start.11
  252.6 1.3 copy-start.16
  253.9 6.9 %copy-start.21 = (s32[1,3,2]{1,2,0:T(2,128)S(1)}, s32[1,3,2]{1,2,0:T(2,128)}, u32[]{:S(2)}) copy-start(s32[1,3,2]{1,2,0:T(2,128)} %param.9) | copy-start | bytes 76
  260.7 346.2 %all-gather.15.cloned.1.call-start = ((), (), s32[]{:S(2)}) async-start(), calls=%async_computation.3 | async-start | bytes 9437184 | tf_op jit(solution)/shard_map/all_gather | solution.py:50
  388.0 39.9 %slice-start.2 = ((s8[8388608]{0:T(1024)(128)(4,1)}), s8[4194304]{0:T(1024)(128)(4,1)S(1)}, s32[]{:S(2)}) async-start(s8[8388608]{0:T(1024)(128)(4,1)} %bitcast.144), calls=%async_computation.6 | async-start | bytes 8388608
  388.0 39.8 %slice-start.3 = ((s8[8388608]{0:T(1024)(128)(4,1)}), s8[4194304]{0:T(1024)(128)(4,1)S(1)}, s32[]{:S(2)}) async-start(s8[8388608]{0:T(1024)(128)(4,1)} %bitcast.144), calls=%async_computation.7 | async-start | bytes 8388608
  388.0 8.0 %collective-permute-start.1 = (bf16[32,1024]{1,0:T(8,128)(2,1)S(1)}, bf16[32,1024]{1,0:T(8,128)(2,1)S(1)}, u32[]{:S(2)}, u32[]{:S(2)}) collective-permute-start(bf16[32,1024]{1,0:T(8,128)(2,1)S(1)} %add_convert_fusion.3), channel_id=1, source_target_pairs={{8,0},{16,8},{24,16},{9,1},{17,9},{25,17},{10,2},{18,10},{26,18},{... | collective-permute-start | bytes 196616 | tf_op jit(solution)/shard_map/ppermute | solution.py:14
  396.1 34.2 %copy-start.8 = (f32[256,4096]{1,0:T(8,128)}, f32[256,4096]{1,0:T(8,128)S(1)}, u32[]{:S(2)}) copy-start(f32[256,4096]{1,0:T(8,128)S(1)} %fusion.26) | copy-start | bytes 12582916
  437.1 7.2 %copy-start.1 = (f32[256,4096]{1,0:T(8,128)S(1)}, f32[256,4096]{1,0:T(8,128)}, u32[]{:S(2)}) copy-start(f32[256,4096]{1,0:T(8,128)} %copy-done) | copy-start | bytes 12582916
  451.2 7.2 %copy-start.2 = (f32[256,4096]{1,0:T(8,128)S(1)}, f32[256,4096]{1,0:T(8,128)}, u32[]{:S(2)}) copy-start(f32[256,4096]{1,0:T(8,128)} %copy-done) | copy-start | bytes 12582916
  464.9 7.3 %copy-start.5 = (f32[256,4096]{1,0:T(8,128)S(1)}, f32[256,4096]{1,0:T(8,128)}, u32[]{:S(2)}) copy-start(f32[256,4096]{1,0:T(8,128)} %copy-done.4) | copy-start | bytes 12582916
  464.9 7.3 %copy-start.12 = (bf16[256,1024]{1,0:T(8,128)(2,1)S(1)}, bf16[256,1024]{1,0:T(8,128)(2,1)}, u32[]{:S(2)}) copy-start(bf16[256,1024]{1,0:T(8,128)(2,1)} %copy-done.11) | copy-start | bytes 1572868
  478.7 7.4 %copy-start.6 = (f32[256,4096]{1,0:T(8,128)S(1)}, f32[256,4096]{1,0:T(8,128)}, u32[]{:S(2)}) copy-start(f32[256,4096]{1,0:T(8,128)} %copy-done.4) | copy-start | bytes 12582916
  478.7 7.4 %copy-start.13 = (bf16[256,1024]{1,0:T(8,128)(2,1)S(1)}, bf16[256,1024]{1,0:T(8,128)(2,1)}, u32[]{:S(2)}) copy-start(bf16[256,1024]{1,0:T(8,128)(2,1)} %copy-done.11) | copy-start | bytes 1572868
  492.6 6.4 %copy-start.9 = (f32[256,4096]{1,0:T(8,128)S(1)}, f32[256,4096]{1,0:T(8,128)}, u32[]{:S(2)}) copy-start(f32[256,4096]{1,0:T(8,128)} %copy-done.8) | copy-start | bytes 12582916
  506.0 6.5 %copy-start.10 = (f32[256,4096]{1,0:T(8,128)S(1)}, f32[256,4096]{1,0:T(8,128)}, u32[]{:S(2)}) copy-start(f32[256,4096]{1,0:T(8,128)} %copy-done.8) | copy-start | bytes 12582916
  538.6 10.1 %copy-start.17 = (bf16[256,4096]{1,0:T(8,128)(2,1)S(1)}, bf16[256,4096]{1,0:T(8,128)(2,1)}, u32[]{:S(2)}) copy-start(bf16[256,4096]{1,0:T(8,128)(2,1)} %copy-done.16) | copy-start | bytes 6291460
  548.7 9.4 %copy-start.7 = (f32[256,4096]{1,0:T(8,128)S(1)}, f32[256,4096]{1,0:T(8,128)}, u32[]{:S(2)}) copy-start(f32[256,4096]{1,0:T(8,128)} %copy-done.4) | copy-start | bytes 12582916
  548.7 9.4 %copy-start.14 = (bf16[256,1024]{1,0:T(8,128)(2,1)S(1)}, bf16[256,1024]{1,0:T(8,128)(2,1)}, u32[]{:S(2)}) copy-start(bf16[256,1024]{1,0:T(8,128)(2,1)} %copy-done.11) | copy-start | bytes 1572868
  558.1 8.2 %copy-start.3 = (f32[256,4096]{1,0:T(8,128)S(1)}, f32[256,4096]{1,0:T(8,128)}, u32[]{:S(2)}) copy-start(f32[256,4096]{1,0:T(8,128)} %copy-done) | copy-start | bytes 12582916
Sparse Core Ops, SparseCore 0:
  16.2 47.6 all-gather.8
  82.2 123.5 all-gather.10
  260.8 122.7 all-gather.12
  437.2 123.1 all-gather.14
